TPU v7x, 32 devices: a whole 2x2x4 slice. The times are simulated.
32 devices in a mesh: lat: 4 (over x, core), lon: 8 (over z, y).
Axes of the slice: x: 2, y: 2, z: 4, core: 2. Of those that a mesh axis runs over, the one named last changes fastest.
Arguments:
- prediction_fields: float32 [4, 69, 360, 512], P(None, None, 'lon', 'lat'), may hold values from -16 to 16
- verifying_state: float32 [69, 360, 512], P(None, 'lon', 'lat'), may hold values from -16 to 16
- normal_state: float32 [69, 360, 512], P(None, 'lon', 'lat'), may hold values from -16 to 16
- evaluated_point_flag: int32 [360, 512], P('lon', 'lat'), may hold values 0 or 1
- parallels_each_strip: int32 [4], replicated, may hold values from 1 to 128, 361 in all
Outputs:
- parallel_quadratic_error: float32 [4, 69, 512], P(None, None, 'lat')
- parallel_systematic_error: float32 [4, 69, 512], P(None, None, 'lat')
- parallel_pattern_skill: float32 [4, 69, 512], P(None, None, 'lat')
- rmse: float32 [4, 69], replicated
- systematic_error: float32 [4, 69], replicated
- pattern_skill: float32 [4, 69], replicated
Inputs may be any that keep to these rules, and one draw needn't show every extreme that they name: `parallels_each_strip`: they sum to 361, and some band holds exactly 128 rows.
All inputs are finite; a program needn't handle non-finite values.
Results may differ from a plain program's by a relative error of at most 0.00002.
Values sent between devices are 32-bit elements.
A program may use at most 64 MiB of HBM per device.

v0:
```python
import jax
import jax.numpy as jnp
from jax import lax
from jax.sharding import PartitionSpec as P

MEAN_ROWS = 90
minimum_divisor = 0.1


def stacked_metrics(totals, horizon_tally, quantity_tally, grid_point_tally):
    block_rows = horizon_tally * quantity_tally
    width = totals.shape[1]
    error_power_two = (
        totals[:block_rows].reshape(horizon_tally, quantity_tally, width) / grid_point_tally
    )
    prediction_error = (
        totals[block_rows : 2 * block_rows].reshape(horizon_tally, quantity_tally, width)
        / grid_point_tally
    )
    paired_anomaly_term = (
        totals[2 * block_rows : 3 * block_rows].reshape(horizon_tally, quantity_tally, width)
        / grid_point_tally
    )
    predicted_spread_sum = (
        totals[3 * block_rows : 4 * block_rows].reshape(horizon_tally, quantity_tally, width)
        / grid_point_tally
    )
    observed_dispersion = (
        totals[4 * block_rows :].reshape(1, quantity_tally, width) / grid_point_tally
    )
    divisor_term = jnp.sqrt(
        jnp.maximum(predicted_spread_sum, minimum_divisor)
        * jnp.maximum(observed_dispersion, minimum_divisor)
    )
    return (error_power_two, prediction_error, paired_anomaly_term / divisor_term)


def local(
    prediction_fields, verifying_state, normal_state, evaluated_point_flag, parallels_each_strip
):
    horizon_tally, quantity_tally, zonal_circle_size, parallel_index = prediction_fields.shape
    lat_bands = lax.axis_size("lat")
    lon_spokes = lax.axis_size("lon")
    lat_total = MEAN_ROWS * lat_bands + 1
    lon_total = zonal_circle_size * lon_spokes
    band_index = lax.axis_index("lat")
    band_ids = jnp.arange(lat_bands, dtype=jnp.int32)
    first_row = jnp.sum(jnp.where(band_ids < band_index, parallels_each_strip, 0))
    band_filled = jnp.sum(jnp.where(band_ids == band_index, parallels_each_strip, 0))
    slot_ids = jnp.arange(parallel_index, dtype=jnp.int32)
    inside_band = slot_ids < band_filled
    angles = jnp.pi * jnp.arange(lat_total, dtype=jnp.float32) / (lat_total - 1)
    normalizer = jnp.sum(jnp.sin(angles))
    row_angle = jnp.pi * (first_row + slot_ids).astype(jnp.float32) / (lat_total - 1)
    area_factors = jnp.where(inside_band, jnp.sin(row_angle) * lat_total / normalizer, 0.0)
    retain_filter = (
        evaluated_point_flag.astype(jnp.float32) * inside_band.astype(jnp.float32)[None, :]
    )
    observed_anomaly = verifying_state - normal_state
    predicted_anomaly = prediction_fields - normal_state[None]
    mistake_field = predicted_anomaly - observed_anomaly[None]
    retained_entries = retain_filter[None, None]
    block_rows = horizon_tally * quantity_tally
    partial_value = jnp.concatenate(
        [
            jnp.sum(retained_entries * mistake_field * mistake_field, axis=2).reshape(
                block_rows, parallel_index
            ),
            jnp.sum(retained_entries * mistake_field, axis=2).reshape(block_rows, parallel_index),
            jnp.sum(retained_entries * predicted_anomaly * observed_anomaly[None], axis=2).reshape(
                block_rows, parallel_index
            ),
            jnp.sum(retained_entries * predicted_anomaly * predicted_anomaly, axis=2).reshape(
                block_rows, parallel_index
            ),
            jnp.sum(retain_filter[None] * observed_anomaly * observed_anomaly, axis=1),
        ],
        axis=0,
    )
    grand = lax.psum(jnp.sum(partial_value * area_factors, axis=1), ("lat", "lon"))
    zonal = lax.psum(partial_value, "lon")
    error_power_two, prediction_error, covariance_sum = stacked_metrics(
        zonal, horizon_tally, quantity_tally, float(lon_total)
    )
    total_square, total_offset, total_agree = stacked_metrics(
        grand[:, None], horizon_tally, quantity_tally, float(lat_total * lon_total)
    )
    rmse = jnp.sqrt(jnp.maximum(total_square[:, :, 0], minimum_divisor))
    return (
        error_power_two,
        prediction_error,
        covariance_sum,
        rmse,
        total_offset[:, :, 0],
        total_agree[:, :, 0],
    )


def solution(mesh):
    in_specs = (
        P(None, None, "lon", "lat"),
        P(None, "lon", "lat"),
        P(None, "lon", "lat"),
        P("lon", "lat"),
        P(),
    )
    out_specs = (P(None, None, "lat"), P(None, None, "lat"), P(None, None, "lat"), P(), P(), P())
    return jax.shard_map(local, mesh=mesh, in_specs=in_specs, out_specs=out_specs, check_vma=False)
```

profile of v0, /device:TPU:0, one launch (start us, length us, event | category | flops | bytes accessed | tf_op | source)
XLA Modules:
  0.0 119.7 jit_solution(12313264060658802673)
XLA Ops:
  7.2 0.0 copy-start.4
  7.2 0.6 sine_reduce_fusion
  7.8 1.3 %fusion.10 = (s32[]{:T(128)}, s32[]{:T(128)}) fusion(s32[4]{0:T(128)} %param.9, s32[]{:T(128)S(6)} %axis_index.15), kind=kLoop, calls=%fused_computation.33 | loop fusion | flops 22 | bytes 28 | tf_op jit(solution)/shard_map/reduce_sum | solution.py:48
  9.1 0.6 compare_convert_fusion
  9.8 0.0 copy-start
  9.8 0.0 copy-start.3
  9.8 1.9 %copy.18 = f32[69,45,128]{2,1,0:T(8,128)S(1)} copy(f32[69,45,128]{2,0,1:T(8,128)} %param.7) | data formatting | bytes 3179520 | tf_op args[2]
  11.7 0.0 copy-done.4
  11.7 0.0 copy-done
  11.8 0.5 copy-done.3
  12.2 0.0 copy-start.1
  12.2 0.3 fusion.3
  12.5 0.3 copy.19
  12.9 2.1 %copy-done.1 = f32[4,69,45,128]{3,0,2,1:T(4,128)S(1)} copy-done((f32[4,69,45,128]{3,0,2,1:T(4,128)S(1)}, f32[4,69,45,128]{3,0,2,1:T(4,128)}, u32[]{:S(2)}) %copy-start.1) | copy-done | bytes 6359064
  15.0 10.1 %fusion.1 = (f32[4,69,128]{2,0,1:T(4,128)S(1)}, f32[4,69,128]{2,0,1:T(4,128)S(1)}, f32[4,69,128]{2,0,1:T(4,128)S(1)}, f32[4,69,128]{2,0,1:T(4,128)S(1)}) fusion(f32[4,69,45,128]{3,0,2,1:T(4,128)S(1)} %copy-done.1, f32[69,45,128]{2,1,0:T(8,128)S(1)} %copy.19, f32[69,45,128]{2,1,0:T(8,128)S(1)} %copy.18, f32[45,128]{1,0:T(8,128)S(1)} %convert_multiply_fusion), kind=kLoop, calls=%fused_computation.5 | loop fusion | flops 17346048 | bytes 10126848 | tf_op jit(solution)/shard_map/reduce_sum | solution.py:70
  25.3 2.0 %compare_select_fusion.2 = f32[128]{0:T(128)S(1)} fusion(f32[]{:T(128)} %sine_reduce_fusion, s32[]{:T(128)} %get-tuple-element.22, s32[]{:T(128)} %get-tuple-element.23), kind=kLoop, calls=%fused_computation.30 | loop fusion | flops 896 | bytes 524 | tf_op jit(solution)/shard_map/jit(_where)/select_n | solution.py:55
  27.3 0.7 concatenate.3
  27.9 0.0 copy-start.2
  27.9 0.2 multiply_reduce_fusion.1
  28.2 0.0 all-reduce.2.cloned.1.call-start
  28.2 0.5 copy-done.2
  28.7 0.2 all-reduce.2.cloned.1.call-update
  28.9 42.2 %psum.15 = f32[1173]{0:T(1024)S(1)} all-reduce(f32[1173]{0:T(1024)S(1)} %multiply_reduce_fusion.1), channel_id=1, replica_groups=mesh['lat'=4,'lon'=8] {'lat','lon'}, use_global_device_ids=true, to_apply=%region_10.11 | all-reduce | flops 1173 | bytes 9384 | tf_op jit(solution)/shard_map/psum | solution.py:80
  71.1 0.1 fusion.6
  71.2 0.1 div.94
  71.3 0.1 max.48
  71.4 0.7 div.92
  72.0 0.7 sqrt.14
  72.7 0.1 fusion.11
  72.8 0.6 rsqrt_multiply_fusion.1
  73.4 35.3 %all-reduce.2.cloned.1.call-done = f32[1173,128]{1,0:T(8,128)} async-done(((f32[1173,128]{1,0:T(8,128)}), f32[1173,128]{1,0:T(8,128)}) %all-reduce.2.cloned.1.call-update) | async-done | bytes 600592 | tf_op jit(solution)/shard_map/psum | solution.py:81
  108.7 1.2 fusion.4
  109.9 0.8 fusion.5
  110.7 0.7 copy.26
  111.4 0.7 copy.24
  112.1 0.7 copy.25
  (14 shorter events, 0.2 us)
Async XLA Ops:
  7.2 4.6 %copy-start.4 = (s32[45,128]{1,0:T(8,128)S(1)}, s32[45,128]{1,0:T(8,128)}, u32[]{:S(2)}) copy-start(s32[45,128]{1,0:T(8,128)} %param.8) | copy-start | bytes 69124
  9.8 2.0 %copy-start = (f32[69,45,128]{2,0,1:T(8,128)S(1)}, f32[69,45,128]{2,0,1:T(8,128)}, u32[]{:S(2)}) copy-start(f32[69,45,128]{2,0,1:T(8,128)} %param.7) | copy-start | bytes 4769284
  9.8 2.4 %copy-start.3 = (f32[69,45,128]{2,0,1:T(8,128)S(1)}, f32[69,45,128]{2,0,1:T(8,128)}, u32[]{:S(2)}) copy-start(f32[69,45,128]{2,0,1:T(8,128)} %param.6) | copy-start | bytes 4769284
  12.2 2.8 %copy-start.1 = (f32[4,69,45,128]{3,0,2,1:T(4,128)S(1)}, f32[4,69,45,128]{3,0,2,1:T(4,128)}, u32[]{:S(2)}) copy-start(f32[4,69,45,128]{3,0,2,1:T(4,128)} %param.5) | copy-start | bytes 19077124
  27.9 0.8 copy-start.2
  28.2 80.5 %all-reduce.2.cloned.1.call-start = ((), (), s32[]{:S(2)}) async-start(), calls=%async_computation | async-start | bytes 1204224 | tf_op jit(solution)/shard_map/psum | solution.py:81
Sparse Core Ops, SparseCore 0:
  32.4 76.1 all-reduce.1
where the time goes:
time: 120 us
  blocking collectives  42.2 us (35%)
  waiting for transfers between devices  35.5 us (30%)
  other arithmetic  18 us (15%)
  between operations  14.2 us (12%)
  local copies, waits for them, and re-layouts  9.77 us (8%)
    psum x1, blocking collectives, local(): lax.psum(jnp.sum(partial_value * area_factors, axis=1), ('lat', 'lon'))  42.2 us
    psum x1, waiting for transfers between devices, local(): zonal = lax.psum(partial_value, 'lon')  35.3 us
    reduce_sum x1, other arithmetic, local(): jnp.sum(retained_entries * predicted_anomaly * observed_anomaly[None], ax...  10.1 us
    unnamed x14, local copies, waits for them, and re-layouts  7.14 us
  transfers between devices with their start and end apart: 1, of which 1 were waited for; matrix products, arithmetic and copies ran while one was open for 2% of the time, Pallas kernels for 0%

commit v1 on v0

--- a/solution.py
+++ b/solution.py
@@ -78,7 +78,9 @@
         axis=0,
     )
     grand = lax.psum(jnp.sum(partial_value * area_factors, axis=1), ("lat", "lon"))
-    zonal = lax.psum(partial_value, "lon")
+    zonal = partial_value
+    for hop in (1, 2, 4):
+        zonal = zonal + lax.ppermute(zonal, "lon", [(dev, dev ^ hop) for dev in range(8)])
     error_power_two, prediction_error, covariance_sum = stacked_metrics(
         zonal, horizon_tally, quantity_tally, float(lon_total)
     )

time: 120 us -> 109 us (0.908)
  between operations: 14.2 us -> 0.84 us
  starting transfers between devices: 0.04 us -> 6.24 us
  blocking collectives: 42.2 us -> 40.4 us
  other arithmetic: 18 us -> 16.3 us
    ppermute x0 -> x3, waiting for transfers between devices: none -> 35.7 us  [local(): lax.ppermute(zonal, 'lon', [(dev, dev ^ hop) for dev in range(8)])]
    psum x1 -> x0, waiting for transfers between devices: 35.3 us -> none  [local(): zonal = lax.psum(partial_value, 'lon')]
    ppermute x0 -> x3, starting transfers between devices: none -> 6.24 us  [local(): lax.ppermute(zonal, 'lon', [(dev, dev ^ hop) for dev in range(8)])]
    psum x1, blocking collectives: 42.2 us -> 40.4 us  [local(): lax.psum(jnp.sum(partial_value * area_factors, axis=1), ('lat', 'lon'))]
    unnamed x14 -> x12, local copies, waits for them, and re-layouts: 7.14 us -> 6.64 us
  transfers between devices with their start and end apart: 1 -> 3, of which waited for: 1 -> 2; matrix products, arithmetic and copies ran while one was open for 2% -> 4% of each run, Pallas kernels for 0% -> 0%
where the time goes in v1:
time: 109 us
  blocking collectives  40.4 us (37%)
  waiting for transfers between devices  35.7 us (33%)
  other arithmetic  16.3 us (15%)
  local copies, waits for them, and re-layouts  9.27 us (9%)
  starting transfers between devices  6.24 us (6%)
    psum x1, blocking collectives, local(): lax.psum(jnp.sum(partial_value * area_factors, axis=1), ('lat', 'lon'))  40.4 us
    ppermute x3, waiting for transfers between devices, local(): lax.ppermute(zonal, 'lon', [(dev, dev ^ hop) for dev in range(8)])  35.7 us
    reduce_sum x1, other arithmetic, local(): jnp.sum(retained_entries * predicted_anomaly * observed_anomaly[None], ax...  10.2 us
    unnamed x12, local copies, waits for them, and re-layouts  6.64 us
    ppermute x3, starting transfers between devices, local(): lax.ppermute(zonal, 'lon', [(dev, dev ^ hop) for dev in range(8)])  6.24 us
  transfers between devices with their start and end apart: 3, of which 2 were waited for; matrix products, arithmetic and copies ran while one was open for 4% of the time, Pallas kernels for 0%

profile of v1, /device:TPU:0, one launch (start us, length us, event | category | flops | bytes accessed | tf_op | source)
XLA Modules:
  0.0 108.8 jit_solution(2865313707658058743)
XLA Ops:
  0.6 0.0 copy-start.3
  0.6 1.3 %fusion.10 = (s32[]{:T(128)}, s32[]{:T(128)}) fusion(s32[4]{0:T(128)} %param.9, s32[]{:T(128)S(6)} %axis_index.15), kind=kLoop, calls=%fused_computation.33 | loop fusion | flops 22 | bytes 28 | tf_op jit(solution)/shard_map/reduce_sum | solution.py:48
  1.9 0.6 compare_convert_fusion
  2.6 0.0 copy-start
  2.6 0.0 copy-start.2
  2.6 1.9 %copy.18 = f32[69,45,128]{2,1,0:T(8,128)S(1)} copy(f32[69,45,128]{2,0,1:T(8,128)} %param.7) | data formatting | bytes 3179520 | tf_op args[2]
  4.5 0.0 copy-done.3
  4.6 0.0 copy-done
  4.6 0.5 copy-done.2
  5.0 0.0 copy-start.1
  5.0 0.3 fusion.3
  5.4 0.3 copy.19
  5.7 2.2 %copy-done.1 = f32[4,69,45,128]{3,0,2,1:T(4,128)S(1)} copy-done((f32[4,69,45,128]{3,0,2,1:T(4,128)S(1)}, f32[4,69,45,128]{3,0,2,1:T(4,128)}, u32[]{:S(2)}) %copy-start.1) | copy-done | bytes 6359064
  7.8 10.2 %fusion.1 = (f32[4,69,128]{2,0,1:T(4,128)S(1)}, f32[4,69,128]{2,0,1:T(4,128)S(1)}, f32[4,69,128]{2,0,1:T(4,128)S(1)}, f32[4,69,128]{2,0,1:T(4,128)S(1)}) fusion(f32[4,69,45,128]{3,0,2,1:T(4,128)S(1)} %copy-done.1, f32[69,45,128]{2,1,0:T(8,128)S(1)} %copy.19, f32[69,45,128]{2,1,0:T(8,128)S(1)} %copy.18, f32[45,128]{1,0:T(8,128)S(1)} %convert_multiply_fusion), kind=kLoop, calls=%fused_computation.5 | loop fusion | flops 17346048 | bytes 10126848 | tf_op jit(solution)/shard_map/reduce_sum | solution.py:70
  18.2 0.7 concatenate.3
  18.9 3.1 %collective-permute-start = (f32[1173,128]{1,0:T(8,128)S(1)}, f32[1173,128]{1,0:T(8,128)S(1)}, u32[]{:S(2)}, u32[]{:S(2)}) collective-permute-start(f32[1173,128]{1,0:T(8,128)S(1)} %concatenate.3), channel_id=1, source_target_pairs={{0,1},{1,0},{2,3},{3,2},{4,5},{5,4},{6,7},{7,6},{8,9},{9,8},{10,11... | collective-permute-start | bytes 1801736 | tf_op jit(solution)/shard_map/ppermute | solution.py:83
  21.9 0.6 sine_reduce_fusion
  22.6 2.0 %compare_select_fusion.2 = f32[128]{0:T(128)S(1)} fusion(f32[]{:T(128)} %sine_reduce_fusion, s32[]{:T(128)} %get-tuple-element.22, s32[]{:T(128)} %get-tuple-element.23), kind=kLoop, calls=%fused_computation.30 | loop fusion | flops 896 | bytes 524 | tf_op jit(solution)/shard_map/jit(_where)/select_n | solution.py:55
  24.6 11.0 %collective-permute-done = f32[1173,128]{1,0:T(8,128)S(1)} collective-permute-done((f32[1173,128]{1,0:T(8,128)S(1)}, f32[1173,128]{1,0:T(8,128)S(1)}, u32[]{:S(2)}, u32[]{:S(2)}) %collective-permute-start) | collective-permute-done | bytes 600608 | tf_op jit(solution)/shard_map/ppermute | solution.py:83
  35.5 0.2 multiply_reduce_fusion.1
  35.8 1.9 %collective-permute-start.1 = (f32[1173,128]{1,0:T(8,128)S(1)}, f32[1173,128]{1,0:T(8,128)S(1)}, u32[]{:S(2)}, u32[]{:S(2)}) collective-permute-start(f32[1173,128]{1,0:T(8,128)S(1)} %get-tuple-element.27), channel_id=1, source_target_pairs={{0,2},{1,3},{2,0},{3,1},{4,6},{5,7},{6,4},{7,5},{8,10},{9,11},{10,... | collective-permute-start | bytes 1801736 | tf_op jit(solution)/shard_map/ppermute | solution.py:83
  37.6 40.4 %psum.7 = f32[1173]{0:T(1024)S(1)} all-reduce(f32[1173]{0:T(1024)S(1)} %get-tuple-element.26), channel_id=1, replica_groups=mesh['lat'=4,'lon'=8] {'lat','lon'}, use_global_device_ids=true, to_apply=%region_9.10 | all-reduce | flops 1173 | bytes 9384 | tf_op jit(solution)/shard_map/psum | solution.py:80
  78.1 0.0 collective-permute-done.1
  78.1 0.1 add.22
  78.1 1.3 %collective-permute-start.2 = (f32[1173,128]{1,0:T(8,128)S(1)}, f32[1173,128]{1,0:T(8,128)S(1)}, u32[]{:S(2)}, u32[]{:S(2)}) collective-permute-start(f32[1173,128]{1,0:T(8,128)S(1)} %add.22), channel_id=1, source_target_pairs={{0,4},{1,5},{2,6},{3,7},{4,0},{5,1},{6,2},{7,3},{8,12},{9,13},{10,... | collective-permute-start | bytes 1801736 | tf_op jit(solution)/shard_map/ppermute | solution.py:83
  79.5 0.1 fusion.6
  79.5 0.1 div.94
  79.6 0.1 max.48
  79.7 0.7 div.92
  80.4 0.7 sqrt.14
  81.0 0.1 fusion.11
  81.1 0.6 rsqrt_multiply_fusion.1
  81.7 24.7 %collective-permute-done.2 = f32[1173,128]{1,0:T(8,128)S(1)} collective-permute-done((f32[1173,128]{1,0:T(8,128)S(1)}, f32[1173,128]{1,0:T(8,128)S(1)}, u32[]{:S(2)}, u32[]{:S(2)}) %collective-permute-start.2) | collective-permute-done | bytes 600608 | tf_op jit(solution)/shard_map/ppermute | solution.py:83
  106.4 0.1 add.23
  106.5 0.1 fusion.4
  106.6 0.7 copy.26
  107.4 0.7 copy.24
  108.1 0.7 copy.25
  (15 shorter events, 0.2 us)
Async XLA Ops:
  0.6 3.9 %copy-start.3 = (s32[45,128]{1,0:T(8,128)S(1)}, s32[45,128]{1,0:T(8,128)}, u32[]{:S(2)}) copy-start(s32[45,128]{1,0:T(8,128)} %param.8) | copy-start | bytes 69124
  2.6 2.0 %copy-start = (f32[69,45,128]{2,0,1:T(8,128)S(1)}, f32[69,45,128]{2,0,1:T(8,128)}, u32[]{:S(2)}) copy-start(f32[69,45,128]{2,0,1:T(8,128)} %param.7) | copy-start | bytes 4769284
  2.6 2.4 %copy-start.2 = (f32[69,45,128]{2,0,1:T(8,128)S(1)}, f32[69,45,128]{2,0,1:T(8,128)}, u32[]{:S(2)}) copy-start(f32[69,45,128]{2,0,1:T(8,128)} %param.6) | copy-start | bytes 4769284
  5.0 2.8 %copy-start.1 = (f32[4,69,45,128]{3,0,2,1:T(4,128)S(1)}, f32[4,69,45,128]{3,0,2,1:T(4,128)}, u32[]{:S(2)}) copy-start(f32[4,69,45,128]{3,0,2,1:T(4,128)} %param.5) | copy-start | bytes 19077124
  18.9 16.7 %collective-permute-start = (f32[1173,128]{1,0:T(8,128)S(1)}, f32[1173,128]{1,0:T(8,128)S(1)}, u32[]{:S(2)}, u32[]{:S(2)}) collective-permute-start(f32[1173,128]{1,0:T(8,128)S(1)} %concatenate.3), channel_id=1, source_target_pairs={{0,1},{1,0},{2,3},{3,2},{4,5},{5,4},{6,7},{7,6},{8,9},{9,8},{10,11... | collective-permute-start | bytes 1801736 | tf_op jit(solution)/shard_map/ppermute | solution.py:83
  35.8 42.3 %collective-permute-start.1 = (f32[1173,128]{1,0:T(8,128)S(1)}, f32[1173,128]{1,0:T(8,128)S(1)}, u32[]{:S(2)}, u32[]{:S(2)}) collective-permute-start(f32[1173,128]{1,0:T(8,128)S(1)} %get-tuple-element.27), channel_id=1, source_target_pairs={{0,2},{1,3},{2,0},{3,1},{4,6},{5,7},{6,4},{7,5},{8,10},{9,11},{10,... | collective-permute-start | bytes 1801736 | tf_op jit(solution)/shard_map/ppermute | solution.py:83
  78.1 28.3 %collective-permute-start.2 = (f32[1173,128]{1,0:T(8,128)S(1)}, f32[1173,128]{1,0:T(8,128)S(1)}, u32[]{:S(2)}, u32[]{:S(2)}) collective-permute-start(f32[1173,128]{1,0:T(8,128)S(1)} %add.22), channel_id=1, source_target_pairs={{0,4},{1,5},{2,6},{3,7},{4,0},{5,1},{6,2},{7,3},{8,12},{9,13},{10,... | collective-permute-start | bytes 1801736 | tf_op jit(solution)/shard_map/ppermute | solution.py:83

commit v2 on v0

--- a/solution.py
+++ b/solution.py
@@ -77,7 +77,7 @@
         ],
         axis=0,
     )
-    grand = lax.psum(jnp.sum(partial_value * area_factors, axis=1), ("lat", "lon"))
+    grand = lax.psum(lax.psum(jnp.sum(partial_value * area_factors, axis=1), "lon"), "lat")
     zonal = lax.psum(partial_value, "lon")
     error_power_two, prediction_error, covariance_sum = stacked_metrics(
         zonal, horizon_tally, quantity_tally, float(lon_total)

time: 120 us -> 120 us (level)
  blocking collectives: 42.2 us -> 29.2 us
  waiting for transfers between devices: 35.5 us -> 48.5 us
    psum x1, waiting for transfers between devices: 35.3 us -> 48.4 us  [local(): zonal = lax.psum(partial_value, 'lon')]
    psum x1 -> x2, blocking collectives: 42.2 us -> 29.2 us  [the longest x1 23.4 us: local(): lax.psum(jnp.sum(partial_value * area_factors, axis=1), 'lon')]
where the time goes in v2:
time: 120 us
  waiting for transfers between devices  48.5 us (40%)
  blocking collectives  29.2 us (24%)
  other arithmetic  18 us (15%)
  between operations  14.2 us (12%)
  local copies, waits for them, and re-layouts  9.77 us (8%)
    psum x1, waiting for transfers between devices, local(): zonal = lax.psum(partial_value, 'lon')  48.4 us
    psum x1, blocking collectives, local(): lax.psum(jnp.sum(partial_value * area_factors, axis=1), 'lon')  23.4 us
    reduce_sum x1, other arithmetic, local(): jnp.sum(retained_entries * predicted_anomaly * observed_anomaly[None], ax...  10.1 us
    unnamed x14, local copies, waits for them, and re-layouts  7.14 us
    psum x1, blocking collectives, local(): lax.psum(lax.psum(jnp.sum(partial_value * area_factors, axis=1), 'lon'),...  5.77 us
  transfers between devices with their start and end apart: 1, of which 1 were waited for; matrix products, arithmetic and copies ran while one was open for 2% of the time, Pallas kernels for 0%

profile of v2, /device:TPU:0, one launch (start us, length us, event | category | flops | bytes accessed | tf_op | source)
XLA Modules:
  0.0 119.7 jit_solution(7372593002769524436)
XLA Ops:
  7.2 0.0 copy-start.4
  7.2 0.6 sine_reduce_fusion
  7.8 1.3 %fusion.10 = (s32[]{:T(128)}, s32[]{:T(128)}) fusion(s32[4]{0:T(128)} %param.9, s32[]{:T(128)S(6)} %axis_index.15), kind=kLoop, calls=%fused_computation.33 | loop fusion | flops 22 | bytes 28 | tf_op jit(solution)/shard_map/reduce_sum | solution.py:48
  9.1 0.6 compare_convert_fusion
  9.8 0.0 copy-start
  9.8 0.0 copy-start.3
  9.8 1.9 %copy.18 = f32[69,45,128]{2,1,0:T(8,128)S(1)} copy(f32[69,45,128]{2,0,1:T(8,128)} %param.7) | data formatting | bytes 3179520 | tf_op args[2]
  11.7 0.0 copy-done.4
  11.7 0.0 copy-done
  11.8 0.5 copy-done.3
  12.2 0.0 copy-start.1
  12.2 0.3 fusion.3
  12.5 0.3 copy.19
  12.9 2.1 %copy-done.1 = f32[4,69,45,128]{3,0,2,1:T(4,128)S(1)} copy-done((f32[4,69,45,128]{3,0,2,1:T(4,128)S(1)}, f32[4,69,45,128]{3,0,2,1:T(4,128)}, u32[]{:S(2)}) %copy-start.1) | copy-done | bytes 6359064
  15.0 10.1 %fusion.1 = (f32[4,69,128]{2,0,1:T(4,128)S(1)}, f32[4,69,128]{2,0,1:T(4,128)S(1)}, f32[4,69,128]{2,0,1:T(4,128)S(1)}, f32[4,69,128]{2,0,1:T(4,128)S(1)}) fusion(f32[4,69,45,128]{3,0,2,1:T(4,128)S(1)} %copy-done.1, f32[69,45,128]{2,1,0:T(8,128)S(1)} %copy.19, f32[69,45,128]{2,1,0:T(8,128)S(1)} %copy.18, f32[45,128]{1,0:T(8,128)S(1)} %convert_multiply_fusion), kind=kLoop, calls=%fused_computation.5 | loop fusion | flops 17346048 | bytes 10126848 | tf_op jit(solution)/shard_map/reduce_sum | solution.py:70
  25.3 2.0 %compare_select_fusion.2 = f32[128]{0:T(128)S(1)} fusion(f32[]{:T(128)} %sine_reduce_fusion, s32[]{:T(128)} %get-tuple-element.22, s32[]{:T(128)} %get-tuple-element.23), kind=kLoop, calls=%fused_computation.30 | loop fusion | flops 896 | bytes 524 | tf_op jit(solution)/shard_map/jit(_where)/select_n | solution.py:55
  27.3 0.7 concatenate.3
  27.9 0.0 copy-start.2
  27.9 0.2 multiply_reduce_fusion.1
  28.2 0.0 all-reduce.2.cloned.1.call-start
  28.2 0.5 copy-done.2
  28.7 0.2 all-reduce.2.cloned.1.call-update
  28.9 23.4 %psum.22 = f32[1173]{0:T(1024)S(1)} all-reduce(f32[1173]{0:T(1024)S(1)} %multiply_reduce_fusion.1), channel_id=1, replica_groups=mesh['lat'=4,'lon'=8] {'lon'}, use_global_device_ids=true, to_apply=%region_10.11 | all-reduce | flops 1173 | bytes 9384 | tf_op jit(solution)/shard_map/psum | solution.py:80
  52.4 5.8 %psum.23 = f32[1173]{0:T(1024)S(1)} all-reduce(f32[1173]{0:T(1024)S(1)} %psum.22), channel_id=1, replica_groups=mesh['lat'=4,'lon'=8] {'lat'}, use_global_device_ids=true, to_apply=%region_11.12 | all-reduce | flops 1173 | bytes 9384 | tf_op jit(solution)/shard_map/psum | solution.py:80
  58.1 0.1 fusion.6
  58.2 0.1 div.94
  58.3 0.1 max.48
  58.4 0.7 div.92
  59.1 0.7 sqrt.14
  59.7 0.1 fusion.11
  59.8 0.6 rsqrt_multiply_fusion.1
  60.4 48.4 %all-reduce.2.cloned.1.call-done = f32[1173,128]{1,0:T(8,128)} async-done(((f32[1173,128]{1,0:T(8,128)}), f32[1173,128]{1,0:T(8,128)}) %all-reduce.2.cloned.1.call-update) | async-done | bytes 600592 | tf_op jit(solution)/shard_map/psum | solution.py:81
  108.7 1.2 fusion.4
  110.0 0.8 fusion.5
  110.8 0.7 copy.26
  111.5 0.7 copy.24
  112.2 0.7 copy.25
  (14 shorter events, 0.2 us)
Async XLA Ops:
  7.2 4.6 %copy-start.4 = (s32[45,128]{1,0:T(8,128)S(1)}, s32[45,128]{1,0:T(8,128)}, u32[]{:S(2)}) copy-start(s32[45,128]{1,0:T(8,128)} %param.8) | copy-start | bytes 69124
  9.8 2.0 %copy-start = (f32[69,45,128]{2,0,1:T(8,128)S(1)}, f32[69,45,128]{2,0,1:T(8,128)}, u32[]{:S(2)}) copy-start(f32[69,45,128]{2,0,1:T(8,128)} %param.7) | copy-start | bytes 4769284
  9.8 2.4 %copy-start.3 = (f32[69,45,128]{2,0,1:T(8,128)S(1)}, f32[69,45,128]{2,0,1:T(8,128)}, u32[]{:S(2)}) copy-start(f32[69,45,128]{2,0,1:T(8,128)} %param.6) | copy-start | bytes 4769284
  12.2 2.8 %copy-start.1 = (f32[4,69,45,128]{3,0,2,1:T(4,128)S(1)}, f32[4,69,45,128]{3,0,2,1:T(4,128)}, u32[]{:S(2)}) copy-start(f32[4,69,45,128]{3,0,2,1:T(4,128)} %param.5) | copy-start | bytes 19077124
  27.9 0.8 copy-start.2
  28.2 80.5 %all-reduce.2.cloned.1.call-start = ((), (), s32[]{:S(2)}) async-start(), calls=%async_computation | async-start | bytes 1204224 | tf_op jit(solution)/shard_map/psum | solution.py:81
Sparse Core Ops, SparseCore 0:
  32.4 76.2 all-reduce.1
